TPU v7x, 256 devices: a whole 4x4x8 slice. The times are simulated.
256 devices in a mesh: ep: 64 (over z, y, core), fsdp: 4 (over x).
Axes of the slice: x: 4, y: 4, z: 8, core: 2. Of those that a mesh axis runs over, the one named last changes fastest.
Arguments:
- train_gate: float32 [64, 2048, 1024], P('ep', 'fsdp'), may hold values from -0.1875 to 0.1875
- other_gate: float32 [64, 2048, 1024], P('ep', 'fsdp'), may hold values from -0.125 to 0.125
- train_up: float32 [64, 2048, 1024], P('ep', 'fsdp'), may hold values from -0.1875 to 0.1875
- other_up: float32 [64, 2048, 1024], P('ep', 'fsdp'), may hold values from -0.125 to 0.125
- mix_share: float32 [64], P('ep'), may hold values from 0.2 to 0.8
- router_weight: float32 [2048, 64], P('fsdp', 'ep'), may hold values from -0.125 to 0.125
- router_gain: float32 [2048], P('fsdp'), may hold values from 0.25 to 1.75
Outputs:
- ready_gate: bfloat16 [64, 2048, 1024], P('ep')
- ready_up: bfloat16 [64, 2048, 1024], P('ep')
- scale_gate: float32 [64, 1024], P('ep')
- scale_up: float32 [64, 1024], P('ep')
- serve_router: bfloat16 [2048, 64], replicated
All inputs are finite; a program needn't handle non-finite values. Where the computation divides by a largest or mean magnitude, that divisor is 1e-20 or more.
Results may differ from a plain program's by a relative error of at most 0.001.
Values may be sent and summed in bfloat16 or wider, within the bound.
A program may use at most 64 MiB of HBM per device.

v0:
```python
import jax
import jax.numpy as jnp
from jax import lax
from jax.sharding import PartitionSpec as P


def sent_to_all(array, axis):
    length = lax.axis_size(axis)
    return lax.all_to_all(
        jnp.broadcast_to(array[None], (length, *array.shape)), axis, 0, 0, tiled=True
    )


def of_everyone(array, axis):
    everything = sent_to_all(array, axis)
    return jnp.max(everything, axis=0)


def together(arrays, axis):
    ends = [0]
    for a in arrays:
        ends.append(ends[-1] + a.size)
    subtotal = of_everyone(jnp.concatenate([a.ravel() for a in arrays]), axis)
    return tuple((subtotal[b:e].reshape(a.shape) for a, b, e in zip(arrays, ends, ends[1:])))


def side_by_side(arrays, axis, dim, along):
    widths = [a.shape[along] for a in arrays]
    both = jnp.concatenate(arrays, axis=along)
    out = lax.all_gather(both, axis, axis=dim, tiled=True)
    return tuple(jnp.split(out, [sum(widths[:k]) for k in range(1, len(widths))], axis=along))


def joined_along(pieces, dim):
    pieces = jnp.moveaxis(pieces, 0, dim)
    dims = pieces.shape
    return pieces.reshape(*dims[:dim], dims[dim] * dims[dim + 1], *dims[dim + 2 :])


def gathered_copies(array, axis, dim):
    pieces = sent_to_all(array, axis)
    return joined_along(pieces, dim)


def per_device(train_gate, other_gate, train_up, other_up, mix_share, router_weight, router_gain):
    latest_gate = (
        mix_share[:, None, None] * train_gate + (1.0 - mix_share[:, None, None]) * other_gate
    )
    latest_up = mix_share[:, None, None] * train_up + (1.0 - mix_share[:, None, None]) * other_up
    scale_gate, scale_up = together(
        (jnp.max(jnp.abs(latest_gate), axis=1), jnp.max(jnp.abs(latest_up), axis=1)), "fsdp"
    )
    narrow_gate, narrow_up = (
        (latest_gate / jnp.expand_dims(scale_gate, 1)).astype(jnp.bfloat16),
        (latest_up / jnp.expand_dims(scale_up, 1)).astype(jnp.bfloat16),
    )
    ready_gate, ready_up = side_by_side((narrow_gate, narrow_up), "fsdp", 1, 0)
    part_router = (router_weight * router_gain[:, None]).astype(jnp.bfloat16)
    row_router = lax.all_gather(part_router, "fsdp", axis=0, tiled=True)
    serve_router = gathered_copies(row_router, "ep", 1)
    return (ready_gate, ready_up, scale_gate, scale_up, serve_router)


def solution(mesh):
    placed = (
        P("ep", "fsdp", None),
        P("ep", "fsdp", None),
        P("ep", "fsdp", None),
        P("ep", "fsdp", None),
        P("ep"),
        P("fsdp", "ep"),
        P("fsdp"),
    )
    return jax.shard_map(
        per_device,
        mesh=mesh,
        in_specs=placed,
        out_specs=(P("ep", None, None), P("ep", None, None), P("ep", None), P("ep", None), P()),
        check_vma=False,
    )
```

profile of v0, /device:TPU:1, one launch (start us, length us, event | category | flops | bytes accessed | tf_op | source)
XLA Modules:
  0.0 127.2 jit_solution(10108246183193982940)
XLA Ops:
  7.2 0.0 all-gather.2.cloned.1.call-start
  7.9 0.0 copy-start
  7.9 0.0 copy-start.1
  7.9 2.6 %abs_reduce_fusion.1 = f32[1024]{0:T(1024)S(1)} fusion(f32[1,512,1024]{2,1,0:T(8,128)} %param.8, f32[]{:T(128)} %bitcast.1, f32[1,512,1024]{2,1,0:T(8,128)} %param.7, f32[]{:T(128)} %bitcast.13), kind=kLoop, calls=%fused_computation.5 | loop fusion | flops 2620416 | bytes 4198408 | tf_op jit(solution)/shard_map/reduce_max | solution.py:51
  10.5 0.2 copy-done
  10.7 0.6 copy-done.1
  11.3 0.3 abs_reduce_fusion
  11.7 8.9 %all_to_all.11 = f32[4,1,2048]{2,1,0:T(1,128)S(1)} all-to-all(f32[4,1,2048]{2,1,0:T(1,128)S(1)} %broadcast_in_dim.8), channel_id=1, replica_groups=mesh['ep'=64,'fsdp'=4] {'fsdp'}, dimensions={0} | all-to-all | bytes 65536 | tf_op jit(solution)/shard_map/all_to_all | solution.py:9
  20.7 0.0 copy-start.2
  20.7 0.0 copy-start.3
  20.7 4.0 %divide_convert_fusion = (bf16[1,512,1024]{2,1,0:T(8,128)(2,1)S(1)}, bf16[1,512,1024]{2,1,0:T(8,128)(2,1)S(1)}) fusion(f32[1024]{0:T(1024)S(1)} %get-tuple-element.8, f32[1,512,1024]{2,1,0:T(8,128)S(1)} %copy-done, f32[]{:T(128)} %bitcast.1, f32[1,512,1024]{2,1,0:T(8,128)} %param.9, f32[]{:T(128)} %bitcast.15, f32[1024]{0:T(1024)S(1)} %get-tuple-element.7, ...), kind=kLoop, calls=%fused_computation.1 | loop fusion | flops 5242880 | bytes 10493960 | tf_op jit(solution)/shard_map/convert_element_type | solution.py:55
  24.6 0.0 copy-done.2
  24.7 0.0 copy-done.3
  24.7 1.5 %pad_maximum_fusion = bf16[2,512,1024]{2,1,0:T(8,128)(2,1)} fusion(bf16[1,512,1024]{2,1,0:T(8,128)(2,1)S(1)} %get-tuple-element.9, bf16[1,512,1024]{2,1,0:T(8,128)(2,1)S(1)} %get-tuple-element.10), kind=kLoop, calls=%fused_computation | loop fusion | flops 1048576 | bytes 4194304 | tf_op jit(solution)/shard_map/concatenate | solution.py:29
  26.2 0.0 copy-start.4
  26.2 0.0 copy-start.5
  26.2 0.0 all-gather.2.cloned.1.call-update
  26.2 0.7 copy-done.4
  26.9 0.0 copy-done.5
  26.9 8.1 %all_gather.7 = bf16[2048,1]{0,1:T(2,128)(2,1)S(1)} all-gather(bf16[512,1]{0,1:T(2,128)(2,1)S(1)} %multiply_convert_fusion), channel_id=1, replica_groups=mesh['ep'=64,'fsdp'=4] {'fsdp'}, dimensions={0}, use_global_device_ids=true | all-gather | bytes 5120 | tf_op jit(solution)/shard_map/all_gather | solution.py:59
  35.0 0.3 broadcast_bitcast_fusion
  35.3 0.5 broadcast.11
  35.8 2.2 %reduce.4 = bf16[64,2048]{1,0:T(8,128)(2,1)S(1)} reduce(bf16[64,1,2048]{2,1,0:T(2,128)(2,1)S(1)} %broadcast_bitcast_fusion, bf16[]{:T(256)} %broadcast.11), dimensions={1}, to_apply=%broadcast_bitcast_fusion.reduce_sub_computation | reduce | bytes 524290
  38.0 0.2 reshape.52
  38.2 28.9 %all_to_all.12 = bf16[64,2,1024]{2,1,0:T(2,128)(2,1)S(1)} all-to-all(bf16[64,2,1024]{2,1,0:T(2,128)(2,1)S(1)} %reshape.52), channel_id=1, replica_groups=mesh['ep'=64,'fsdp'=4] {'ep'}, dimensions={0} | all-to-all | bytes 524288 | tf_op jit(solution)/shard_map/all_to_all | solution.py:9
  67.1 0.2 reshape.53
  67.3 0.9 copy.20
  68.2 46.1 %all-gather.2.cloned.1.call-done = bf16[2,2048,1024]{2,1,0:T(8,128)(2,1)} async-done(((bf16[2,512,1024]{2,1,0:T(8,128)(2,1)}), bf16[2,2048,1024]{2,1,0:T(8,128)(2,1)}) %all-gather.2.cloned.1.call-update) | async-done | bytes 8388624 | tf_op jit(solution)/shard_map/all_gather | solution.py:30
  114.3 6.0 %fusion = (bf16[1,2048,1024]{2,1,0:T(8,128)(2,1)}, bf16[1,2048,1024]{2,1,0:T(8,128)(2,1)}) fusion(bf16[2,2048,1024]{2,1,0:T(8,128)(2,1)} %all-gather.2.cloned.1.call-done), kind=kLoop, calls=%fused_computation.10 | loop fusion | bytes 16777216 | tf_op jit(solution)/shard_map/split | solution.py:31
  (6 shorter events, 0.1 us)
Async XLA Ops:
  7.2 107.2 %all-gather.2.cloned.1.call-start = ((), (), s32[]{:S(2)}) async-start(), calls=%async_computation.2 | async-start | bytes 10485760 | tf_op jit(solution)/shard_map/all_gather | solution.py:30
  7.9 2.9 %copy-start = (f32[1,512,1024]{2,1,0:T(8,128)S(1)}, f32[1,512,1024]{2,1,0:T(8,128)}, u32[]{:S(2)}) copy-start(f32[1,512,1024]{2,1,0:T(8,128)} %param.10) | copy-start | bytes 6291460
  7.9 3.5 %copy-start.1 = (f32[1,512,1024]{2,1,0:T(8,128)S(1)}, f32[1,512,1024]{2,1,0:T(8,128)}, u32[]{:S(2)}) copy-start(f32[1,512,1024]{2,1,0:T(8,128)} %param.9) | copy-start | bytes 6291460
  20.7 4.0 %copy-start.2 = (f32[1024]{0:T(1024)}, f32[1024]{0:T(1024)S(1)}, u32[]{:S(2)}) copy-start(f32[1024]{0:T(1024)S(1)} %get-tuple-element.7) | copy-start | bytes 12292
  20.7 4.0 %copy-start.3 = (f32[1024]{0:T(1024)}, f32[1024]{0:T(1024)S(1)}, u32[]{:S(2)}) copy-start(f32[1024]{0:T(1024)S(1)} %get-tuple-element.8) | copy-start | bytes 12292
  26.2 0.7 copy-start.4
  26.2 0.7 copy-start.5
Sparse Core Ops, SparseCore 0:
  26.3 87.9 all-gather.1
where the time goes:
time: 127 us
  waiting for transfers between devices  46.1 us (36%)
  blocking collectives  46 us (36%)
  between operations  14.8 us (12%)
  other arithmetic  10.6 us (8%)
  local copies, waits for them, and re-layouts  9.61 us (8%)
    all_gather x1, waiting for transfers between devices, side_by_side(): out = lax.all_gather(both, axis, axis=dim, tiled=True)  46.1 us
    all_to_all x2, blocking collectives, sent_to_all(): lax.all_to_all(jnp.broadcast_to(array[None], (length, *array.shape)), axi...  37.9 us
    all_gather x1, blocking collectives, per_device(): row_router = lax.all_gather(part_router, 'fsdp', axis=0, tiled=True)  8.13 us
    split x1, local copies, waits for them, and re-layouts, side_by_side(): jnp.split(out, [sum(widths[:k]) for k in range(1, len(widths))], axis=along)  6.02 us
    convert_element_type x1, other arithmetic, per_device(): (latest_up / jnp.expand_dims(scale_up, 1)).astype(jnp.bfloat16)  3.95 us
    unnamed x16, local copies, waits for them, and re-layouts  2.71 us
    reduce_max x1, other arithmetic, per_device(): jnp.max(jnp.abs(latest_gate), axis=1)  2.63 us
  transfers between devices with their start and end apart: 1, of which 1 were waited for; matrix products, arithmetic and copies ran while one was open for 3% of the time, Pallas kernels for 0%

commit v1 on v0

--- a/solution.py
+++ b/solution.py
@@ -2,6 +2,14 @@
 import jax.numpy as jnp
 from jax import lax
 from jax.sharding import PartitionSpec as P
+
+
+def gather_from_all(value, axis, dim):
+    peers = lax.axis_size(axis)
+    repeats = [peers if d == dim else 1 for d in range(value.ndim)]
+    return lax.all_to_all(
+        jnp.tile(value, repeats), axis, split_axis=dim, concat_axis=dim, tiled=True
+    )
 
 
 def sent_to_all(array, axis):
@@ -56,7 +64,7 @@
     )
     ready_gate, ready_up = side_by_side((narrow_gate, narrow_up), "fsdp", 1, 0)
     part_router = (router_weight * router_gain[:, None]).astype(jnp.bfloat16)
-    row_router = lax.all_gather(part_router, "fsdp", axis=0, tiled=True)
+    row_router = gather_from_all(part_router, "fsdp", 0)
     serve_router = gathered_copies(row_router, "ep", 1)
     return (ready_gate, ready_up, scale_gate, scale_up, serve_router)
 

time: 127 us -> 127 us (level)
  blocking collectives: 46 us -> 43.2 us
  waiting for transfers between devices: 46.1 us -> 48.2 us
    all_gather x1 -> x0, blocking collectives: 8.13 us -> none  [per_device(): row_router = lax.all_gather(part_router, 'fsdp', axis=0, tiled=True)]
    all_to_all x0 -> x1, blocking collectives: none -> 6.48 us  [gather_from_all(): lax.all_to_all(jnp.tile(value, repeats), axis, split_axis=dim, concat_axi...]
    all_gather x1, waiting for transfers between devices: 46.1 us -> 48.2 us  [side_by_side(): out = lax.all_gather(both, axis, axis=dim, tiled=True)]
    unnamed x1 -> x2, other arithmetic: 2.15 us -> 2.83 us
    unnamed x16 -> x20, local copies, waits for them, and re-layouts: 2.71 us -> 2.75 us
  transfers between devices with their start and end apart: 1 -> 1, of which waited for: 1 -> 1; matrix products, arithmetic and copies ran while one was open for 3% -> 4% of each run, Pallas kernels for 0% -> 0%
where the time goes in v1:
time: 127 us
  waiting for transfers between devices  48.2 us (38%)
  blocking collectives  43.2 us (34%)
  between operations  14.8 us (12%)
  other arithmetic  11.3 us (9%)
  local copies, waits for them, and re-layouts  9.68 us (8%)
    all_gather x1, waiting for transfers between devices, side_by_side(): out = lax.all_gather(both, axis, axis=dim, tiled=True)  48.2 us
    all_to_all x2, blocking collectives, sent_to_all(): lax.all_to_all(jnp.broadcast_to(array[None], (length, *array.shape)), axi...  36.7 us
    all_to_all x1, blocking collectives, gather_from_all(): lax.all_to_all(jnp.tile(value, repeats), axis, split_axis=dim, concat_axi...  6.48 us
    split x1, local copies, waits for them, and re-layouts, side_by_side(): jnp.split(out, [sum(widths[:k]) for k in range(1, len(widths))], axis=along)  6.02 us
    convert_element_type x1, other arithmetic, per_device(): (latest_up / jnp.expand_dims(scale_up, 1)).astype(jnp.bfloat16)  3.95 us
    unnamed x2, other arithmetic  2.83 us
    unnamed x20, local copies, waits for them, and re-layouts  2.75 us
    reduce_max x1, other arithmetic, per_device(): jnp.max(jnp.abs(latest_gate), axis=1)  2.63 us
  transfers between devices with their start and end apart: 1, of which 1 were waited for; matrix products, arithmetic and copies ran while one was open for 4% of the time, Pallas kernels for 0%

profile of v1, /device:TPU:1, one launch (start us, length us, event | category | flops | bytes accessed | tf_op | source)
XLA Modules:
  0.0 127.2 jit_solution(5256462546767895766)
XLA Ops:
  7.2 0.0 all-gather.2.cloned.1.call-start
  7.9 0.0 copy-start
  7.9 0.0 copy-start.1
  7.9 2.6 %abs_reduce_fusion.1 = f32[1024]{0:T(1024)S(1)} fusion(f32[1,512,1024]{2,1,0:T(8,128)} %param.8, f32[]{:T(128)} %bitcast.1, f32[1,512,1024]{2,1,0:T(8,128)} %param.7, f32[]{:T(128)} %bitcast.19), kind=kLoop, calls=%fused_computation.5 | loop fusion | flops 2620416 | bytes 4198408 | tf_op jit(solution)/shard_map/reduce_max | solution.py:59
  10.5 0.2 copy-done
  10.7 0.6 copy-done.1
  11.3 0.3 abs_reduce_fusion
  11.7 8.9 %all_to_all.17 = f32[4,1,2048]{2,1,0:T(1,128)S(1)} all-to-all(f32[4,1,2048]{2,1,0:T(1,128)S(1)} %broadcast_in_dim.8), channel_id=1, replica_groups=mesh['ep'=64,'fsdp'=4] {'fsdp'}, dimensions={0} | all-to-all | bytes 65536 | tf_op jit(solution)/shard_map/all_to_all | solution.py:17
  20.7 0.0 copy-start.2
  20.7 0.0 copy-start.3
  20.7 4.0 %divide_convert_fusion = (bf16[1,512,1024]{2,1,0:T(8,128)(2,1)S(1)}, bf16[1,512,1024]{2,1,0:T(8,128)(2,1)S(1)}) fusion(f32[1024]{0:T(1024)S(1)} %get-tuple-element.8, f32[1,512,1024]{2,1,0:T(8,128)S(1)} %copy-done, f32[]{:T(128)} %bitcast.1, f32[1,512,1024]{2,1,0:T(8,128)} %param.9, f32[]{:T(128)} %bitcast.21, f32[1024]{0:T(1024)S(1)} %get-tuple-element.7, ...), kind=kLoop, calls=%fused_computation.1 | loop fusion | flops 5242880 | bytes 10493960 | tf_op jit(solution)/shard_map/convert_element_type | solution.py:63
  24.6 0.0 copy-done.2
  24.7 0.0 copy-done.3
  24.7 1.5 %pad_maximum_fusion = bf16[2,512,1024]{2,1,0:T(8,128)(2,1)} fusion(bf16[1,512,1024]{2,1,0:T(8,128)(2,1)S(1)} %get-tuple-element.9, bf16[1,512,1024]{2,1,0:T(8,128)(2,1)S(1)} %get-tuple-element.10), kind=kLoop, calls=%fused_computation | loop fusion | flops 1048576 | bytes 4194304 | tf_op jit(solution)/shard_map/concatenate | solution.py:37
  26.2 0.0 copy-start.4
  26.2 0.0 copy-start.5
  26.2 0.0 all-gather.2.cloned.1.call-update
  26.2 0.7 copy-done.4
  26.9 0.0 copy-done.5
  26.9 0.5 broadcast.16
  27.4 0.7 reduce.7
  28.1 6.5 %all_to_all.18 = bf16[4,2,256]{2,1,0:T(2,128)(2,1)S(1)} all-to-all(bf16[4,2,256]{2,1,0:T(2,128)(2,1)S(1)} %reshape.62), channel_id=1, replica_groups=mesh['ep'=64,'fsdp'=4] {'fsdp'}, dimensions={0} | all-to-all | bytes 8192 | tf_op jit(solution)/shard_map/all_to_all | solution.py:10
  34.7 0.3 broadcast_bitcast_fusion
  34.9 2.2 %reduce.8 = bf16[64,2048]{1,0:T(8,128)(2,1)S(1)} reduce(bf16[64,1,2048]{2,1,0:T(2,128)(2,1)S(1)} %broadcast_bitcast_fusion, bf16[]{:T(256)} %broadcast.16), dimensions={1}, to_apply=%broadcast_bitcast_fusion.reduce_sub_computation | reduce | bytes 524290
  37.1 0.2 reshape.64
  37.3 27.8 %all_to_all.19 = bf16[64,2,1024]{2,1,0:T(2,128)(2,1)S(1)} all-to-all(bf16[64,2,1024]{2,1,0:T(2,128)(2,1)S(1)} %reshape.64), channel_id=1, replica_groups=mesh['ep'=64,'fsdp'=4] {'ep'}, dimensions={0} | all-to-all | bytes 524288 | tf_op jit(solution)/shard_map/all_to_all | solution.py:17
  65.1 0.2 reshape.65
  65.3 0.9 copy.21
  66.1 48.2 %all-gather.2.cloned.1.call-done = bf16[2,2048,1024]{2,1,0:T(8,128)(2,1)} async-done(((bf16[2,512,1024]{2,1,0:T(8,128)(2,1)}), bf16[2,2048,1024]{2,1,0:T(8,128)(2,1)}) %all-gather.2.cloned.1.call-update) | async-done | bytes 8388624 | tf_op jit(solution)/shard_map/all_gather | solution.py:38
  114.3 6.0 %fusion = (bf16[1,2048,1024]{2,1,0:T(8,128)(2,1)}, bf16[1,2048,1024]{2,1,0:T(8,128)(2,1)}) fusion(bf16[2,2048,1024]{2,1,0:T(8,128)(2,1)} %all-gather.2.cloned.1.call-done), kind=kLoop, calls=%fused_computation.10 | loop fusion | bytes 16777216 | tf_op jit(solution)/shard_map/split | solution.py:39
  (10 shorter events, 0.2 us)
Async XLA Ops:
  7.2 107.2 %all-gather.2.cloned.1.call-start = ((), (), s32[]{:S(2)}) async-start(), calls=%async_computation.3 | async-start | bytes 10485760 | tf_op jit(solution)/shard_map/all_gather | solution.py:38
  7.9 2.9 %copy-start = (f32[1,512,1024]{2,1,0:T(8,128)S(1)}, f32[1,512,1024]{2,1,0:T(8,128)}, u32[]{:S(2)}) copy-start(f32[1,512,1024]{2,1,0:T(8,128)} %param.10) | copy-start | bytes 6291460
  7.9 3.5 %copy-start.1 = (f32[1,512,1024]{2,1,0:T(8,128)S(1)}, f32[1,512,1024]{2,1,0:T(8,128)}, u32[]{:S(2)}) copy-start(f32[1,512,1024]{2,1,0:T(8,128)} %param.9) | copy-start | bytes 6291460
  20.7 4.0 %copy-start.2 = (f32[1024]{0:T(1024)}, f32[1024]{0:T(1024)S(1)}, u32[]{:S(2)}) copy-start(f32[1024]{0:T(1024)S(1)} %get-tuple-element.7) | copy-start | bytes 12292
  20.7 4.0 %copy-start.3 = (f32[1024]{0:T(1024)}, f32[1024]{0:T(1024)S(1)}, u32[]{:S(2)}) copy-start(f32[1024]{0:T(1024)S(1)} %get-tuple-element.8) | copy-start | bytes 12292
  26.2 0.7 copy-start.4
  26.2 0.7 copy-start.5
Sparse Core Ops, SparseCore 0:
  26.3 87.9 all-gather.1
